TPU v7x, 32 devices: a whole 2x2x4 slice. The times are simulated.
32 devices in a mesh: seq: 8 (over z, x), section: 4 (over y, core).
Axes of the slice: x: 2, y: 2, z: 4, core: 2. Of those that a mesh axis runs over, the one named last changes fastest.
Arguments:
- grad_top: bfloat16 [4, 4096, 2560], P('section', 'seq'), may hold values from -6 to 6
- in_weight: bfloat16 [2560, 2560], P(('seq', 'section')), may hold values from -0.125 to 0.125
- out_weight: bfloat16 [2560, 2560], P(('seq', 'section')), may hold values from -0.125 to 0.125
- gate_branch: bfloat16 [4, 4096, 2560], P('section', 'seq'), may hold values from -6 to 6
- write_vec: bfloat16 [4, 4096, 128], P('section', 'seq'), may hold values from -0.59765625 to 0.59765625
- read_vec: bfloat16 [4, 4096, 128], P('section', 'seq'), may hold values from -6 to 6
- log_decay: float32 [4, 40, 4096], P('section', None, 'seq'), may hold values from -1 to 0
- step_size: float32 [4, 40, 4096], P('section', None, 'seq'), may hold values from 0.005 to 0.05
- skip_gain: float32 [40], replicated, may hold values from 0.5 to 1.5
- visual_pos: int32 [4, 8, 16], P('section', 'seq'), may hold values from 0 to 511, as said below
- visual_count: int32 [4, 8], P('section'), may hold values from 2 to 16, as said below
- visual_owner: int32 [4, 8, 16], P('section'), may hold values from 0 to 7, as said below
- visual_patch: int32 [4, 8, 16], P('section'), may hold values from 0 to 15, as said below
Outputs:
- layer_grads: bfloat16 [4, 4096, 2560], P('section', 'seq')
- patch_grads: bfloat16 [4, 128, 2560], P('section', 'seq')
Inputs may be any that keep to these rules, and one draw needn't show every extreme that they name: `visual_pos`: the 16 positions of one shard are distinct; only the first visual_count of them hold visual tokens. `visual_count`: in every sequence some shard has all 16 slots live. `visual_owner`: of the slots of one shard at most 2 name one owner; in every sequence one owner is named by 2 live slots of every shard. `visual_patch`: slots of one sequence that name the same owner name distinct patches.
All inputs are finite; a program needn't handle non-finite values.
Results may differ from a plain program's by a relative error of at most 0.014.
Values may be sent and summed in bfloat16 or wider, within the bound.
A program may use at most 192 MiB of HBM per device.

v0:
```python
import jax
import jax.numpy as jnp
from jax import lax
from jax.sharding import PartitionSpec as P

GROUP = 256
CAP = 2


exact_mode = lax.Precision.HIGHEST


def entering(x, axis, combine, identity):
    length, index = (lax.axis_size(axis), lax.axis_index(axis))
    everything = jax.tree.map(
        lambda part, kind: lax.all_gather(part.astype(kind), axis), x, (jnp.bfloat16, jnp.bfloat16)
    )
    start = jax.tree.map(
        lambda part, zero: jnp.broadcast_to(jnp.asarray(zero, part.dtype), part.shape), x, identity
    )

    def lap(k, before):
        at = length - 1 - k
        reached = at > index
        new = combine(
            before, jax.tree.map(lambda part, own: part[at].astype(own.dtype), everything, x)
        )
        return jax.tree.map(lambda a, b: jnp.where(reached, a, b), new, before)

    return lax.fori_loop(0, length, lap, start)


def combine_tail(earlier_part, later_part):
    return (
        later_part[0] + earlier_part[0],
        later_part[1] + jnp.exp(later_part[0])[:, None, None] * earlier_part[1],
    )


def body(
    grad_top,
    in_weight,
    out_weight,
    gate_branch,
    write_vec,
    read_vec,
    log_decay,
    step_size,
    skip_gain,
    visual_pos,
    visual_count,
    visual_owner,
    visual_patch,
):
    seq_count = lax.axis_size("seq")
    seq_index = lax.axis_index("seq")
    grad_rows = grad_top[0]
    tok_rows, model_width = grad_rows.shape
    head_count = log_decay.shape[1]
    inner_width = gate_branch.shape[2]
    head_size = inner_width // head_count
    state_width = write_vec.shape[2]
    slot_count = visual_owner.shape[2]
    out_value = jnp.dot(
        grad_rows,
        lax.all_gather(out_weight, ("seq", "section"), axis=0, tiled=True),
        preferred_element_type=jnp.float32,
    )
    block_len = min(GROUP, tok_rows)
    block_total = tok_rows // block_len
    gated = out_value * jax.nn.silu(gate_branch[0].astype(jnp.float32))
    gated_blocks = gated.reshape(block_total, block_len, head_count, head_size)
    write_blocks = write_vec[0].astype(jnp.float32).reshape(block_total, block_len, state_width)
    read_blocks = read_vec[0].astype(jnp.float32).reshape(block_total, block_len, state_width)
    decay_blocks = log_decay[0].reshape(head_count, block_total, block_len).transpose(1, 0, 2)
    step_blocks = step_size[0].reshape(head_count, block_total, block_len).transpose(1, 0, 2)
    cum_blocks = jnp.cumsum(decay_blocks, axis=2)
    scaled = gated_blocks * jnp.exp(cum_blocks).transpose(0, 2, 1)[:, :, :, None]
    contrib_blocks = jnp.einsum("cshp,csn->chpn", scaled, read_blocks, precision=exact_mode)
    block_decays = cum_blocks[:, :, -1]
    leading = jnp.cumsum(block_decays, axis=0) - block_decays
    device_contrib = jnp.einsum(
        "ch,chpn->hpn", jnp.exp(leading), contrib_blocks, precision=exact_mode
    )
    device_decay = jnp.sum(block_decays, axis=0)
    identity = (jnp.zeros_like(device_decay), jnp.zeros_like(device_contrib))
    _, inflow = entering((device_decay, device_contrib), "seq", combine_tail, identity)
    token_locations = jnp.arange(block_len)
    causal = token_locations[None, :] >= token_locations[:, None]

    def block_step(arriving, pieces):
        gated_c, write_c, read_c, cum_c, step_c, contrib_c = pieces
        gram = jnp.dot(write_c, read_c.T, precision=exact_mode)
        log_gap = cum_c[:, None, :] - cum_c[:, :, None]
        mixing = jnp.where(causal[None], jnp.exp(jnp.minimum(log_gap, 0.0)), 0.0) * gram[None]
        within = jnp.einsum("hts,shp->thp", mixing, gated_c, precision=exact_mode)
        tail_decay = jnp.exp(cum_c[:, -1:] - cum_c).T
        from_later = (
            jnp.einsum("hpn,tn->thp", arriving, write_c, precision=exact_mode)
            * tail_decay[:, :, None]
        )
        inner_c = step_c.T[:, :, None] * (within + from_later) + skip_gain[None, :, None] * gated_c
        leaving = contrib_c + jnp.exp(cum_c[:, -1])[:, None, None] * arriving
        return (leaving, inner_c)

    _, inner_blocks = lax.scan(
        block_step,
        inflow,
        (gated_blocks, write_blocks, read_blocks, cum_blocks, step_blocks, contrib_blocks),
        reverse=True,
    )
    inner_grad = inner_blocks.reshape(tok_rows, inner_width).astype(jnp.bfloat16)
    back = lax.dot_general(
        inner_grad,
        lax.all_gather(in_weight, ("seq", "section"), axis=0, tiled=True),
        (((1,), (1,)), ((), ())),
        preferred_element_type=jnp.float32,
    )
    result = (grad_rows.astype(jnp.float32) + back).astype(jnp.bfloat16)
    own_rows = result[visual_pos[0, 0]]
    owner_row = visual_owner[0]
    patch_row = visual_patch[0]
    count_row = visual_count[0]
    slot_ids = jnp.arange(slot_count)
    live_slot = slot_ids[None, :] < count_row[:, None]
    earlier_slot = slot_ids[None, :] < slot_ids[:, None]
    same_owner = (
        (owner_row[:, :, None] == owner_row[:, None, :])
        & live_slot[:, None, :]
        & earlier_slot[None]
    )
    rank_row = jnp.sum(same_owner.astype(jnp.int32), axis=2)
    own_owner = lax.dynamic_index_in_dim(owner_row, seq_index, 0, keepdims=False)
    own_rank = lax.dynamic_index_in_dim(rank_row, seq_index, 0, keepdims=False)
    own_live = lax.dynamic_index_in_dim(live_slot, seq_index, 0, keepdims=False)
    destination = own_owner * CAP + own_rank
    send_columns = jnp.arange(seq_count * CAP)
    send_map = ((send_columns[:, None] == destination[None, :]) & own_live[None, :]).astype(
        jnp.bfloat16
    )
    send_rows = jnp.dot(send_map, own_rows, preferred_element_type=jnp.float32).astype(jnp.bfloat16)
    send_rows = send_rows.reshape(seq_count, CAP, model_width)
    landed = lax.all_to_all(send_rows, "seq", split_axis=0, concat_axis=0, tiled=True)
    mine_mask = live_slot & (owner_row == seq_index)
    column = jnp.arange(seq_count)[:, None] * CAP + rank_row
    patch_count = seq_count * CAP
    patch_hit = (
        (patch_row.reshape(-1)[:, None] == jnp.arange(patch_count)[None, :])
        & mine_mask.reshape(-1)[:, None]
    ).astype(jnp.bfloat16)
    column_hit = (column.reshape(-1)[:, None] == send_columns[None, :]).astype(jnp.bfloat16)
    select = lax.dot_general(
        patch_hit, column_hit, (((0,), (0,)), ((), ())), preferred_element_type=jnp.float32
    ).astype(jnp.bfloat16)
    patches = jnp.dot(
        select, landed.reshape(seq_count * CAP, model_width), preferred_element_type=jnp.float32
    ).astype(jnp.bfloat16)
    return (result[None], patches[None])


def solution(mesh):
    return jax.shard_map(
        body,
        mesh=mesh,
        in_specs=(
            P("section", "seq", None),
            P(("seq", "section"), None),
            P(("seq", "section"), None),
            P("section", "seq", None),
            P("section", "seq", None),
            P("section", "seq", None),
            P("section", None, "seq"),
            P("section", None, "seq"),
            P(),
            P("section", "seq", None),
            P("section", None),
            P("section", None, None),
            P("section", None, None),
        ),
        out_specs=(P("section", "seq", None), P("section", "seq", None)),
        check_vma=False,
    )
```

profile of v0, /device:TPU:0, one launch (start us, length us, event | category | flops | bytes accessed | tf_op | source)
XLA Modules:
  0.0 376.1 jit_solution(11185542998818894503)
XLA Ops:
  7.2 0.7 all-gather.6.cloned.1.call-update
  7.9 0.9 reshape_squeeze.6
  8.9 1.2 reduce-window.6
  10.4 0.2 slice_reduce_fusion.1
  10.9 100.4 %all-gather.6.cloned.1.call-done = bf16[2560,2560]{1,0:T(8,128)(2,1)} async-done(((bf16[80,2560]{1,0:T(8,128)(2,1)}), bf16[2560,2560]{1,0:T(8,128)(2,1)}) %all-gather.6.cloned.1.call-update) | async-done | bytes 13107216 | tf_op jit(solution)/shard_map/all_gather | solution.py:66
  111.3 13.0 %fusion.30 = f32[512,2560]{1,0:T(8,128)} fusion(bf16[2560,2560]{1,0:T(8,128)(2,1)} %all-gather.6.cloned.1.call-done, bf16[1,512,2560]{2,1,0:T(8,128)(2,1)} %param.20, bf16[1,512,2560]{2,1,0:T(8,128)(2,1)} %param.17), kind=kOutput, calls=%fused_computation.45 | convolution fusion | flops 6718750720 | bytes 23592960 | tf_op jit(solution)/shard_map/dot_general | solution.py:64
  124.3 5.9 %copy.66 = f32[512,2560]{0,1:T(8,128)} copy(f32[512,2560]{1,0:T(8,128)} %fusion.30) | data formatting | bytes 10485760 | tf_op jit(solution)/shard_map/mul | solution.py:71
  130.2 7.4 %reshape.198 = f32[2,256,40,64]{1,0,3,2:T(2,128)} reshape(f32[512,2560]{0,1:T(8,128)} %copy.66) | data formatting | bytes 10485760 | tf_op jit(solution)/shard_map/reshape | solution.py:72
  137.6 4.9 %broadcast_multiply_fusion = f32[2,256,40,64]{1,0,3,2:T(2,128)S(1)} fusion(f32[2,256,40,64]{1,0,3,2:T(2,128)} %reshape.198, f32[2,256,40]{1,0,2:T(2,128)S(1)} %copy.67), kind=kLoop, calls=%fused_computation.53 | loop fusion | flops 1310720 | bytes 10567680 | tf_op jit(solution)/shard_map/mul | solution.py:78
  142.5 2.5 fusion.31
  145.0 10.4 %fusion.35 = f32[40,1,64,128]{3,1,2,0:T(1,128)S(1)} fusion(f32[2,40,1,1]{0,2,3,1:T(1,128)S(1)} %copy.74, f32[2,40,64,128]{3,2,1,0:T(8,128)S(1)} %fusion.31), kind=kOutput, calls=%fused_computation.54 | convolution fusion | flops 7864320 | bytes 3932480 | tf_op jit(solution)/shard_map/ch,chpn->hpn/dot_general | solution.py:82
  155.5 0.9 convert_element_type.91
  156.5 0.7 all-gather.8.cloned.1.call-update
  157.2 0.7 dynamic-slice.1
  158.5 0.2 dynamic-update-slice
  158.8 20.5 %all-reduce = bf16[320]{0:T(512)(128)(2,1)S(1)} all-reduce(bf16[320]{0:T(512)(128)(2,1)S(1)} %dynamic-update-slice), channel_id=3, replica_groups=mesh['seq'=8,'section'=4] {'seq'}, use_global_device_ids=true, to_apply=%add | all-reduce | flops 320 | bytes 1280
  179.8 0.3 convert_reduce_fusion
  180.1 61.1 %all-gather.10.cloned.1.call-done = bf16[320,64,128]{2,1,0:T(8,128)(2,1)} async-done(((bf16[40,64,128]{2,1,0:T(8,128)(2,1)}), bf16[320,64,128]{2,1,0:T(8,128)(2,1)}) %all-gather.10.cloned.1.call-update) | async-done | bytes 5242896 | tf_op jit(solution)/shard_map/all_gather | solution.py:16
  241.2 11.8 %while.34 = (s32[]{:T(128)}, f32[40,64,128]{2,1,0:T(8,128)S(1)}, s32[]{:T(128)}, bf16[8,40,64,128]{3,2,1,0:T(8,128)(2,1)}, bf16[8,40]{1,0:T(8,128)(2,1)S(1)}, /*index=5*/s32[]{:T(128)}, s32[]{:T(128)}, s32[]{:T(128)}, s32[]{:T(128)}) while((s32[]{:T(128)}, f32[40,64,128]{2,1,0:T(8,128)S(1)}, s32[]{:T(128)}, ...), condition=%wide.region_5.6_spmd.clone, body=%wide.region_4.5_spmd.clone.sunk | while | flops 1638448 | bytes 3277367 | solution.py:30
  241.2 1.4 fusion.83
  242.7 1.4 fusion.83
  244.2 1.4 fusion.83
  245.6 1.4 fusion.83
  247.1 1.4 fusion.83
  248.6 1.4 fusion.83
  250.0 1.5 fusion.83
  251.6 1.5 fusion.83
  253.0 1.8 broadcast_in_dim.46
  254.8 51.4 %while.33 = (s32[]{:T(128)}, f32[40,64,128]{2,1,0:T(8,128)S(1)}, bf16[2,256,40,64]{1,3,2,0:T(8,128)(2,1)}, f32[2,40,64,128]{3,2,1,0:T(8,128)}, f32[2,40,256]{2,1...) while((s32[]{:T(128)}, f32[40,64,128]{2,1,0:T(8,128)S(1)}, ...), condition=%wide.region_7.8_spmd.clone, body=%wide.region_6.7_spmd.clone.sunk | while | flops 3135055872 | bytes 46313092 | solution.py:106
  254.8 0.4 fusion.80
  255.2 5.3 %constant_dynamic-slice_fusion.9 = f32[1,256,40,64]{1,0,3,2:T(1,128)S(1)} fusion(f32[2,256,40,64]{1,0,3,2:T(2,128)} %get-tuple-element.622, s32[]{:T(128)S(6)} %sub.111), kind=kLoop, calls=%fused_computation.31.clone.1 | loop fusion | bytes 5242884 | tf_op jit(solution)/shard_map/while/body/jit(dynamic_index_in_dim)/dynamic_slice | solution.py:106
  260.6 13.1 %fusion.82 = f32[40,64,256]{2,1,0:T(8,128)} fusion(f32[256,256]{1,0:T(8,128)S(1)} %fusion.80, f32[40,256]{1,0:T(8,128)S(1)} %fusion.81, pred[256,256]{1,0:T(8,128)(4,1)S(1)} %iota_compare_fusion.9, f32[1,256,40,64]{1,0,3,2:T(1,128)S(1)} %constant_dynamic-slice_fusion.9), kind=kOutput, calls=%fused_computation.2.clone.1 | convolution fusion | flops 2023751680 | bytes 5611520 | tf_op jit(solution)/shard_map/while/body/eval_jaxpr/hts,shp->thp/dot_general | solution.py:96
  274.0 6.1 %bitcast_dynamic-update-slice_fusion.2 = bf16[2,256,40,64]{1,3,2,0:T(8,128)(2,1)} fusion(bf16[2,256,40,64]{1,3,2,0:T(8,128)(2,1)} %get-tuple-element.607, s32[]{:T(128)S(6)} %sub.111, f32[40,64,256]{2,1,0:T(8,128)} %fusion.82, f32[1,256,40,64]{1,0,3,2:T(1,128)} %copy-done, f32[40,64,128]{2,1,0:T(8,128)S(1)} %get-tuple-element.606, ...), kind=kOutput, calls=%fused_computation.14.clone.1 | convolution fusion | flops 1009909760 | bytes 9389568 | tf_op jit(solution)/shard_map/while/body/eval_jaxpr/hpn,tn->thp/dot_general | solution.py:99
  280.1 0.3 bitcast_add_fusion.3
  280.4 0.4 fusion.80
  280.8 5.3 %constant_dynamic-slice_fusion.9 = f32[1,256,40,64]{1,0,3,2:T(1,128)S(1)} fusion(f32[2,256,40,64]{1,0,3,2:T(2,128)} %get-tuple-element.622, s32[]{:T(128)S(6)} %sub.111), kind=kLoop, calls=%fused_computation.31.clone.1 | loop fusion | bytes 5242884 | tf_op jit(solution)/shard_map/while/body/jit(dynamic_index_in_dim)/dynamic_slice | solution.py:106
  286.2 13.1 %fusion.82 = f32[40,64,256]{2,1,0:T(8,128)} fusion(f32[256,256]{1,0:T(8,128)S(1)} %fusion.80, f32[40,256]{1,0:T(8,128)S(1)} %fusion.81, pred[256,256]{1,0:T(8,128)(4,1)S(1)} %iota_compare_fusion.9, f32[1,256,40,64]{1,0,3,2:T(1,128)S(1)} %constant_dynamic-slice_fusion.9), kind=kOutput, calls=%fused_computation.2.clone.1 | convolution fusion | flops 2023751680 | bytes 5611520 | tf_op jit(solution)/shard_map/while/body/eval_jaxpr/hts,shp->thp/dot_general | solution.py:96
  299.6 6.1 %bitcast_dynamic-update-slice_fusion.2 = bf16[2,256,40,64]{1,3,2,0:T(8,128)(2,1)} fusion(bf16[2,256,40,64]{1,3,2,0:T(8,128)(2,1)} %get-tuple-element.607, s32[]{:T(128)S(6)} %sub.111, f32[40,64,256]{2,1,0:T(8,128)} %fusion.82, f32[1,256,40,64]{1,0,3,2:T(1,128)} %copy-done, f32[40,64,128]{2,1,0:T(8,128)S(1)} %get-tuple-element.606, ...), kind=kOutput, calls=%fused_computation.14.clone.1 | convolution fusion | flops 1009909760 | bytes 9389568 | tf_op jit(solution)/shard_map/while/body/eval_jaxpr/hpn,tn->thp/dot_general | solution.py:99
  305.7 0.3 bitcast_add_fusion.3
  306.3 4.5 %copy.72 = bf16[2,256,40,64]{1,0,3,2:T(2,128)(2,1)S(1)} copy(bf16[2,256,40,64]{1,3,2,0:T(8,128)(2,1)} %get-tuple-element.352) | data formatting | bytes 5242880 | tf_op jit(solution)/shard_map/convert_element_type | solution.py:112
  310.8 1.9 copy.83
  312.7 27.3 %all-gather.8.cloned.1.call-done = bf16[2560,2560]{1,0:T(8,128)(2,1)} async-done(((bf16[80,2560]{1,0:T(8,128)(2,1)}), bf16[2560,2560]{1,0:T(8,128)(2,1)}) %all-gather.8.cloned.1.call-update) | async-done | bytes 13107216 | tf_op jit(solution)/shard_map/all_gather | solution.py:115
  340.0 13.9 %add_convert_fusion = bf16[512,2560]{1,0:T(8,128)(2,1)} fusion(bf16[512,2560]{0,1:T(8,128)(2,1)} %bitcast.157, bf16[2560,2560]{1,0:T(8,128)(2,1)} %all-gather.8.cloned.1.call-done, bf16[1,512,2560]{2,1,0:T(8,128)(2,1)} %param.17), kind=kOutput, calls=%fused_computation.48 | convolution fusion | flops 6714818560 | bytes 20971520 | tf_op jit(solution)/shard_map/dot_general | solution.py:113
  353.9 2.8 gather_fusion
  356.8 0.7 reshape.200
  357.5 4.0 %all-to-all-start = ((bf16[8,2,2560]{2,1,0:T(2,128)(2,1)}), bf16[8,2,2560]{2,1,0:T(2,128)(2,1)S(1)}, u32[]{:S(2)}, u32[]{:S(2)}) async-start(bf16[8,2,2560]{2,1,0:T(2,128)(2,1)} %reshape.200), calls=%async_computation | async-start | bytes 163840 | tf_op jit(solution)/shard_map/all_to_all | solution.py:143
  361.7 6.8 %all-to-all-done = bf16[8,2,2560]{2,1,0:T(2,128)(2,1)S(1)} async-done(((bf16[8,2,2560]{2,1,0:T(2,128)(2,1)}), bf16[8,2,2560]{2,1,0:T(2,128)(2,1)S(1)}, u32[]{:S(2)}, u32[]{:S(2)}) %all-to-all-start) | async-done | bytes 81952 | tf_op jit(solution)/shard_map/all_to_all | solution.py:143
  368.5 1.0 fusion.33
  (92 shorter events, 2.4 us)
Async XLA Ops:
  7.2 104.1 %all-gather.6.cloned.1.call-start = ((), (), s32[]{:S(2)}) async-start(), calls=%async_computation.1 | async-start | bytes 13516800 | tf_op jit(solution)/shard_map/all_gather | solution.py:66
  7.9 233.3 %all-gather.10.cloned.1.call-start = ((), (), s32[]{:S(2)}) async-start(), calls=%async_computation.3 | async-start | bytes 5898240 | tf_op jit(solution)/shard_map/all_gather | solution.py:16
  137.6 4.9 %copy-start.3 = (bf16[1,512,128]{2,1,0:T(8,128)(2,1)S(1)}, bf16[1,512,128]{2,1,0:T(8,128)(2,1)}, u32[]{:S(2)}) copy-start(bf16[1,512,128]{2,1,0:T(8,128)(2,1)} %param.22) | copy-start | bytes 393220
  145.0 10.4 %copy-start.1 = (f32[2,40,64,128]{3,2,1,0:T(8,128)}, f32[2,40,64,128]{3,2,1,0:T(8,128)S(1)}, u32[]{:S(2)}) copy-start(f32[2,40,64,128]{3,2,1,0:T(8,128)S(1)} %fusion.31) | copy-start | bytes 7864324
  155.4 1.8 copy-start.11
  155.4 23.9 %copy-start.4 = (bf16[1,512,128]{2,1,0:T(8,128)(2,1)S(1)}, bf16[1,512,128]{2,1,0:T(8,128)(2,1)}, u32[]{:S(2)}) copy-start(bf16[1,512,128]{2,1,0:T(8,128)(2,1)} %param.21) | copy-start | bytes 393220
  155.4 24.0 %copy-start.5 = (f32[1,40,512]{2,1,0:T(8,128)S(1)}, f32[1,40,512]{2,1,0:T(8,128)}, u32[]{:S(2)}) copy-start(f32[1,40,512]{2,1,0:T(8,128)} %param.24) | copy-start | bytes 245764
  155.4 24.0 %copy-start.6 = (s32[1,8,16]{2,1,0:T(8,128)S(1)}, s32[1,8,16]{2,1,0:T(8,128)}, u32[]{:S(2)}) copy-start(s32[1,8,16]{2,1,0:T(8,128)} %param.28) | copy-start | bytes 1540
  155.4 24.1 %copy-start.9 = (s32[1,8]{1,0:T(1,128)S(1)}, s32[1,8]{1,0:T(1,128)}, u32[]{:S(2)}) copy-start(s32[1,8]{1,0:T(1,128)} %param.27) | copy-start | bytes 100
  155.4 24.6 %copy-start.10 = (s32[1,1,16]{2,1,0:T(1,128)S(1)}, s32[1,1,16]{2,1,0:T(1,128)}, u32[]{:S(2)}) copy-start(s32[1,1,16]{2,1,0:T(1,128)} %param.26) | copy-start | bytes 196
  156.4 183.6 %all-gather.8.cloned.1.call-start = ((), (), s32[]{:S(2)}) async-start(), calls=%async_computation.2 | async-start | bytes 13516800 | tf_op jit(solution)/shard_map/all_gather | solution.py:115
  253.0 1.8 copy-start.7
  260.5 13.2 %copy-start = (f32[1,256,40,64]{1,0,3,2:T(1,128)}, f32[1,256,40,64]{1,0,3,2:T(1,128)S(1)}, u32[]{:S(2)}) copy-start(f32[1,256,40,64]{1,0,3,2:T(1,128)S(1)} %constant_dynamic-slice_fusion.9) | copy-start | bytes 7864324 | tf_op jit(solution)/shard_map/while
  274.0 6.1 %copy-start.2 = (f32[2,40,64,128]{3,2,1,0:T(8,128)S(1)}, f32[2,40,64,128]{3,2,1,0:T(8,128)}, u32[]{:S(2)}) copy-start(f32[2,40,64,128]{3,2,1,0:T(8,128)} %get-tuple-element.619) | copy-start | bytes 7864324 | tf_op jit(solution)/shard_map/while
  286.1 13.2 %copy-start = (f32[1,256,40,64]{1,0,3,2:T(1,128)}, f32[1,256,40,64]{1,0,3,2:T(1,128)S(1)}, u32[]{:S(2)}) copy-start(f32[1,256,40,64]{1,0,3,2:T(1,128)S(1)} %constant_dynamic-slice_fusion.9) | copy-start | bytes 7864324 | tf_op jit(solution)/shard_map/while
  299.6 6.1 %copy-start.2 = (f32[2,40,64,128]{3,2,1,0:T(8,128)S(1)}, f32[2,40,64,128]{3,2,1,0:T(8,128)}, u32[]{:S(2)}) copy-start(f32[2,40,64,128]{3,2,1,0:T(8,128)} %get-tuple-element.619) | copy-start | bytes 7864324 | tf_op jit(solution)/shard_map/while
  340.0 21.6 %copy-start.8 = (s32[1,8,16]{2,1,0:T(8,128)S(1)}, s32[1,8,16]{2,1,0:T(8,128)}, u32[]{:S(2)}) copy-start(s32[1,8,16]{2,1,0:T(8,128)} %param.29) | copy-start | bytes 1540
  357.5 11.0 %all-to-all-start = ((bf16[8,2,2560]{2,1,0:T(2,128)(2,1)}), bf16[8,2,2560]{2,1,0:T(2,128)(2,1)S(1)}, u32[]{:S(2)}, u32[]{:S(2)}) async-start(bf16[8,2,2560]{2,1,0:T(2,128)(2,1)} %reshape.200), calls=%async_computation | async-start | bytes 163840 | tf_op jit(solution)/shard_map/all_to_all | solution.py:143
Sparse Core Ops, SparseCore 0:
  10.8 100.4 all-gather.5
  156.6 84.6 all-gather.9
  244.1 95.9 all-gather.7
where the time goes:
time: 377 us; the launch traced here: 376 us
  waiting for transfers between devices  197 us (52%)
  matrix products  80.1 us (21%)
  local copies, waits for them, and re-layouts  38.8 us (10%)
  blocking collectives  20.5 us (5%)
  other arithmetic  20.2 us (5%)
  between operations  14.7 us (4%)
  starting transfers between devices  4.11 us (1%)
    all_gather x1, waiting for transfers between devices, body(): lax.all_gather(out_weight, ('seq', 'section'), axis=0, tiled=True)  100 us
    all_gather x1, waiting for transfers between devices, entering(): lax.all_gather(part.astype(kind), axis)  61.1 us
    all_gather x1, waiting for transfers between devices, body(): lax.all_gather(in_weight, ('seq', 'section'), axis=0, tiled=True)  27.3 us
    dot_general x2, matrix products, block_step(): within = jnp.einsum('hts,shp->thp', mixing, gated_c, precision=exact_mode)  26.2 us
    unnamed x1, blocking collectives  20.5 us
    dot_general x1, matrix products, body(): lax.dot_general(inner_grad, lax.all_gather(in_weight, ('seq', 'section'),...  13.9 us
    dot_general x1, matrix products, body(): jnp.dot(grad_rows, lax.all_gather(out_weight, ('seq', 'section'), axis=0,...  13 us
    dot_general x2, matrix products, block_step(): jnp.einsum('hpn,tn->thp', arriving, write_c, precision=exact_mode)  12.2 us
  transfers between devices with their start and end apart: 4, of which 4 were waited for; matrix products, arithmetic and copies ran while one was open for 20% of the time, Pallas kernels for 0%

commit v1 on v0

v1 whole, which is shorter than its diff:
```python
import functools
import jax
import jax.numpy as jnp
from jax import lax
from jax.experimental import pallas as pl
from jax.experimental.pallas import tpu as pltpu
from jax.sharding import Mesh, PartitionSpec as P

BLOCK = 128
LANES = 128
GROUPS = 2
CAP = 2
VMEM_BYTES = 48 * 2**20


def spread(cols, first, heads, head_size):
    rows = cols.shape[0]
    lane = lax.broadcasted_iota(jnp.int32, (rows, heads * head_size), 1)
    out = jnp.broadcast_to(cols[:, first : first + 1], lane.shape)
    for i in range(1, heads):
        col = jnp.broadcast_to(cols[:, first + i : first + i + 1], lane.shape)
        out = jnp.where(lane < i * head_size, out, col)
    return out


def contrib_kernel(heads, head_size, g_ref, col_ref, read_t_ref, out_ref):
    cols = col_ref[0]
    width = heads * head_size
    for j in range(g_ref.shape[1] // width):
        at = slice(j * width, (j + 1) * width)
        scaled = g_ref[:, at].astype(jnp.float32) * spread(cols, j * heads, heads, head_size)
        out_ref[:, at] = jnp.dot(
            read_t_ref[...], scaled.astype(jnp.bfloat16), preferred_element_type=jnp.float32
        ).astype(jnp.bfloat16)


def local_kernel(
    heads, head_size, g_ref, col_ref, row_ref, gram_ref, write_ref, read_t_ref, skip_ref, out_ref
):
    width = heads * head_size
    groups = g_ref.shape[1] // width
    blocks, length, _ = gram_ref.shape
    per = groups * heads
    lane = lax.broadcasted_iota(jnp.int32, (length, width), 1)
    for j in range(groups):
        at = slice(j * width, (j + 1) * width)
        state = None
        for b in range(blocks - 1, -1, -1):
            rows = slice(b * length, (b + 1) * length)
            cols = col_ref[0, rows, :]
            g_b = g_ref[rows, at]
            g_f = g_b.astype(jnp.float32)
            gram = gram_ref[b]
            total = None
            for i in range(heads):
                h = j * heads + i
                gap = row_ref[0, h : h + 1, rows] - cols[:, h : h + 1]
                mixing = (jnp.exp(jnp.minimum(gap, 0.0)) * gram).astype(jnp.bfloat16)
                part = jnp.dot(mixing, g_b, preferred_element_type=jnp.float32)
                total = part if i == 0 else jnp.where(lane < i * head_size, total, part)
            if state is not None:
                later = jnp.dot(
                    write_ref[rows, :],
                    state.astype(jnp.bfloat16),
                    preferred_element_type=jnp.float32,
                )
                total += later * spread(cols, 2 * per + j * heads, heads, head_size)
            step = spread(cols, 3 * per + j * heads, heads, head_size)
            out_ref[rows, at] = step * total + skip_ref[:, at] * g_f
            if b > 0:
                grow = spread(cols, per + j * heads, heads, head_size)
                add = jnp.dot(
                    read_t_ref[:, rows],
                    (g_f * grow).astype(jnp.bfloat16),
                    preferred_element_type=jnp.float32,
                )
                state = add if state is None else add + grow[length - 1 :, :] * state


def finish_kernel(heads, head_size, loc_ref, col_ref, write_ref, state_ref, out_ref):
    cols = col_ref[0]
    width = heads * head_size
    for j in range(loc_ref.shape[1] // width):
        at = slice(j * width, (j + 1) * width)
        later = jnp.dot(write_ref[...], state_ref[:, at], preferred_element_type=jnp.float32)
        out_ref[:, at] = (
            loc_ref[:, at] + later * spread(cols, j * heads, heads, head_size)
        ).astype(jnp.bfloat16)


def by_step(x, per):
    return x.reshape(-1, per, x.shape[1]).transpose(0, 2, 1)


def body(
    grad_top,
    in_weight,
    out_weight,
    gate_branch,
    write_vec,
    read_vec,
    log_decay,
    step_size,
    skip_gain,
    visual_pos,
    visual_count,
    visual_owner,
    visual_patch,
):
    seq_count = lax.axis_size("seq")
    seq_index = lax.axis_index("seq")
    lane_count = lax.axis_size("lane")
    pair_count = lax.axis_size("pair")
    grad_rows = grad_top[0]
    tok_rows, model_width = grad_rows.shape
    head_count = log_decay.shape[1]
    inner_width = gate_branch.shape[2]
    head_size = inner_width // head_count
    state_width = write_vec.shape[2]
    slot_count = visual_owner.shape[2]
    weight_rows = out_weight.shape[0]

    held = lax.all_gather(out_weight, ("seq", "lane"), axis=0, tiled=True)
    in_part, held = lax.optimization_barrier((in_weight, held))
    in_full = lax.all_gather(in_part, ("seq", "lane", "pair"), axis=0, tiled=True)
    pair_index = lax.axis_index("pair")
    grad_cols = grad_rows.reshape(
        tok_rows, seq_count * lane_count, pair_count, weight_rows
    ).transpose(2, 0, 1, 3).reshape(pair_count, tok_rows, -1)
    out_value = jnp.dot(
        lax.dynamic_index_in_dim(grad_cols, pair_index, 0, keepdims=False),
        held,
        preferred_element_type=jnp.float32,
    )
    for shift in range(1, pair_count):
        other = lax.ppermute(
            held, "pair", [((i + shift) % pair_count, i) for i in range(pair_count)]
        )
        source = (pair_index + shift) % pair_count
        out_value += jnp.dot(
            lax.dynamic_index_in_dim(grad_cols, source, 0, keepdims=False),
            other,
            preferred_element_type=jnp.float32,
        )
    gated = (out_value * jax.nn.silu(gate_branch[0].astype(jnp.float32))).astype(jnp.bfloat16)

    length = min(BLOCK, tok_rows)
    blocks = tok_rows // length
    heads = LANES // head_size
    per = GROUPS * heads
    steps = head_count // per
    width = per * head_size
    cum_blocks = jnp.cumsum(log_decay[0].reshape(head_count, blocks, length), axis=2)
    ends = cum_blocks[:, :, -1]
    before = jnp.cumsum(ends, axis=1) - ends
    after = jnp.sum(ends, axis=1, keepdims=True) - before - ends
    device_decay = jnp.sum(ends, axis=1)
    tails = jnp.exp(ends[:, :, None] - cum_blocks)
    flat = (head_count, tok_rows)
    cum = cum_blocks.reshape(flat)
    step_rows = step_size[0]
    lead_cols = by_step(jnp.exp(cum_blocks + before[:, :, None]).reshape(flat), per)
    local_cols = jnp.concatenate(
        [
            by_step(x, per)
            for x in (cum, jnp.exp(cum), tails.reshape(flat), step_rows)
        ],
        axis=2,
    )
    last_cols = by_step(
        step_rows * (tails * jnp.exp(after)[:, :, None]).reshape(flat), per
    )
    cum_rows = cum.reshape(steps, per, tok_rows)
    skip_row = jnp.repeat(skip_gain, head_size)[None, :]
    write_rows = write_vec[0]
    read_rows = read_vec[0]
    read_t = read_rows.T
    gram = jnp.einsum(
        "btn,bsn->bts",
        write_rows.reshape(blocks, length, state_width),
        read_rows.reshape(blocks, length, state_width),
        preferred_element_type=jnp.float32,
    )
    place = jnp.arange(length)
    gram = jnp.where(place[None, None, :] >= place[None, :, None], gram, 0.0)

    wide = pl.BlockSpec((tok_rows, width), lambda i: (0, i))
    state_spec = pl.BlockSpec((state_width, width), lambda i: (0, i))

    def col_spec(x):
        return pl.BlockSpec((1,) + x.shape[1:], lambda i: (i, 0, 0))

    def whole(x):
        return pl.BlockSpec(x.shape, lambda i: (0,) * x.ndim)

    params = pltpu.CompilerParams(vmem_limit_bytes=VMEM_BYTES)
    state_flops = 2 * tok_rows * state_width * inner_width
    contrib = pl.pallas_call(
        functools.partial(contrib_kernel, heads, head_size),
        grid=(steps,),
        out_shape=jax.ShapeDtypeStruct((state_width, inner_width), jnp.bfloat16),
        in_specs=[wide, col_spec(lead_cols), whole(read_t)],
        out_specs=state_spec,
        compiler_params=params,
        cost_estimate=pl.CostEstimate(
            flops=state_flops, bytes_accessed=gated.size * 2, transcendentals=0
        ),
    )(gated, lead_cols, read_t)
    local = pl.pallas_call(
        functools.partial(local_kernel, heads, head_size),
        grid=(steps,),
        out_shape=jax.ShapeDtypeStruct((tok_rows, inner_width), jnp.float32),
        in_specs=[
            wide,
            col_spec(local_cols),
            col_spec(cum_rows),
            whole(gram),
            whole(write_rows),
            whole(read_t),
            pl.BlockSpec((1, width), lambda i: (0, i)),
        ],
        out_specs=wide,
        compiler_params=params,
        cost_estimate=pl.CostEstimate(
            flops=40 * state_flops, bytes_accessed=gated.size * 6, transcendentals=0
        ),
    )(gated, local_cols, cum_rows, gram, write_rows, read_t, skip_row)

    decays = jnp.exp(lax.all_gather(device_decay, "seq"))
    decays = jnp.repeat(decays, head_size, axis=1)
    shares = lax.all_to_all(
        contrib.reshape(seq_count, -1, inner_width), "seq", split_axis=0, concat_axis=0, tiled=True
    ).astype(jnp.float32)
    running = jnp.zeros(shares.shape[1:], jnp.float32)
    arriving = [running]
    for k in range(seq_count - 1, 0, -1):
        running = shares[k] + decays[k][None, :] * running
        arriving.append(running)
    arriving = jnp.stack(arriving[::-1]).astype(jnp.bfloat16)
    inflow = lax.all_to_all(
        arriving, "seq", split_axis=0, concat_axis=0, tiled=True
    ).reshape(state_width, inner_width)

    inner_grad = pl.pallas_call(
        functools.partial(finish_kernel, heads, head_size),
        grid=(steps,),
        out_shape=jax.ShapeDtypeStruct((tok_rows, inner_width), jnp.bfloat16),
        in_specs=[wide, col_spec(last_cols), whole(write_rows), state_spec],
        out_specs=wide,
        compiler_params=params,
        cost_estimate=pl.CostEstimate(
            flops=state_flops, bytes_accessed=gated.size * 6, transcendentals=0
        ),
    )(local, last_cols, write_rows, inflow)
    back = lax.dot_general(
        inner_grad, in_full, (((1,), (1,)), ((), ())), preferred_element_type=jnp.float32
    )
    result = (grad_rows.astype(jnp.float32) + back).astype(jnp.bfloat16)
    own_rows = result[visual_pos[0, 0]]
    owner_row = visual_owner[0]
    patch_row = visual_patch[0]
    count_row = visual_count[0]
    slot_ids = jnp.arange(slot_count)
    live_slot = slot_ids[None, :] < count_row[:, None]
    earlier_slot = slot_ids[None, :] < slot_ids[:, None]
    same_owner = (
        (owner_row[:, :, None] == owner_row[:, None, :])
        & live_slot[:, None, :]
        & earlier_slot[None]
    )
    rank_row = jnp.sum(same_owner.astype(jnp.int32), axis=2)
    own_owner = lax.dynamic_index_in_dim(owner_row, seq_index, 0, keepdims=False)
    own_rank = lax.dynamic_index_in_dim(rank_row, seq_index, 0, keepdims=False)
    own_live = lax.dynamic_index_in_dim(live_slot, seq_index, 0, keepdims=False)
    destination = own_owner * CAP + own_rank
    send_columns = jnp.arange(seq_count * CAP)
    send_map = ((send_columns[:, None] == destination[None, :]) & own_live[None, :]).astype(
        jnp.bfloat16
    )
    send_rows = jnp.dot(send_map, own_rows, preferred_element_type=jnp.float32).astype(jnp.bfloat16)
    send_rows = send_rows.reshape(seq_count, CAP, model_width)
    landed = lax.all_to_all(send_rows, "seq", split_axis=0, concat_axis=0, tiled=True)
    mine_mask = live_slot & (owner_row == seq_index)
    column = jnp.arange(seq_count)[:, None] * CAP + rank_row
    patch_count = seq_count * CAP
    patch_hit = (
        (patch_row.reshape(-1)[:, None] == jnp.arange(patch_count)[None, :])
        & mine_mask.reshape(-1)[:, None]
    ).astype(jnp.bfloat16)
    column_hit = (column.reshape(-1)[:, None] == send_columns[None, :]).astype(jnp.bfloat16)
    select = lax.dot_general(
        patch_hit, column_hit, (((0,), (0,)), ((), ())), preferred_element_type=jnp.float32
    ).astype(jnp.bfloat16)
    patches = jnp.dot(
        select, landed.reshape(seq_count * CAP, model_width), preferred_element_type=jnp.float32
    ).astype(jnp.bfloat16)
    return (result[None], patches[None])


def solution(mesh):
    seq, section = mesh.shape["seq"], mesh.shape["section"]
    pair = 2 if section % 2 == 0 else 1
    split = Mesh(mesh.devices.reshape(seq, section // pair, pair), ("seq", "lane", "pair"))
    section = ("lane", "pair")
    return jax.shard_map(
        body,
        mesh=split,
        in_specs=(
            P(section, "seq", None),
            P(("seq", "lane", "pair"), None),
            P(("seq", "lane", "pair"), None),
            P(section, "seq", None),
            P(section, "seq", None),
            P(section, "seq", None),
            P(section, None, "seq"),
            P(section, None, "seq"),
            P(),
            P(section, "seq", None),
            P(section, None),
            P(section, None, None),
            P(section, None, None),
        ),
        out_specs=(P(section, "seq", None), P(section, "seq", None)),
        check_vma=False,
    )
```

time: 377 us -> 290 us (0.77)
  waiting for transfers between devices: 197 us -> 129 us
  matrix products: 80.1 us -> 29.6 us
  Pallas kernels: 0 us -> 29 us
  starting transfers between devices: 4.11 us -> 13.3 us
  local copies, waits for them, and re-layouts: 38.8 us -> 35 us
    all_gather x3 -> x2, waiting for transfers between devices: 189 us -> 102 us  [the longest x1 102 us: body(): held = lax.all_gather(out_weight, ('seq', 'lane'), axis=0, tiled=True)]
    dot_general x10 -> x4, matrix products: 78.9 us -> 28.4 us  [the longest x1 11.2 us: body(): lax.dot_general(inner_grad, in_full, (((1,), (1,)), ((), ())), preferred_...]
    pallas_call x0 -> x3, Pallas kernels: none -> 29 us  [the longest x1 14.5 us: body(): pl.pallas_call(functools.partial(local_kernel, heads, head_size), grid=(s...]
    all_to_all x0 -> x2, waiting for transfers between devices: none -> 20.1 us  [the longest x1 20.1 us: body(): lax.all_to_all(contrib.reshape(seq_count, -1, inner_width), 'seq', split_...]
    select_n x8 -> x0, other arithmetic: 11.4 us -> none  [lap(): return jax.tree.map(lambda a, b: jnp.where(reached, a, b), new, before)]
    dynamic_slice x10 -> x0, local copies, waits for them, and re-layouts: 10.8 us -> none  [body(): lax.scan(block_step, inflow, (gated_blocks, write_blocks, read_blocks, cu...]
    unnamed x24 -> x65, local copies, waits for them, and re-layouts: 2.87 us -> 12.5 us
    reshape x2 -> x0, local copies, waits for them, and re-layouts: 7.45 us -> none  [the longest x1 7.44 us: body(): gated_blocks = gated.reshape(block_total, block_len, head_count, head_size)]
  transfers between devices with their start and end apart: 4 -> 6, of which waited for: 4 -> 3; matrix products, arithmetic and copies ran while one was open for 20% -> 21% of each run, Pallas kernels for 0% -> 10%
where the time goes in v1:
time: 290 us; the launch traced here: 289 us
  waiting for transfers between devices  129 us (44%)
  local copies, waits for them, and re-layouts  35 us (12%)
  matrix products  29.6 us (10%)
  Pallas kernels  29 us (10%)
  blocking collectives  19.9 us (7%)
  other arithmetic  18.2 us (6%)
  between operations  15.2 us (5%)
  starting transfers between devices  13.3 us (5%)
    all_gather x1, waiting for transfers between devices, body(): held = lax.all_gather(out_weight, ('seq', 'lane'), axis=0, tiled=True)  102 us
    all_to_all x1, waiting for transfers between devices, body(): lax.all_to_all(contrib.reshape(seq_count, -1, inner_width), 'seq', split_...  20.1 us
    unnamed x1, blocking collectives  19.9 us
    pallas_call x1, Pallas kernels, body(): pl.pallas_call(functools.partial(local_kernel, heads, head_size), grid=(s...  14.5 us
    unnamed x65, local copies, waits for them, and re-layouts  12.5 us
    dot_general x1, matrix products, body(): lax.dot_general(inner_grad, in_full, (((1,), (1,)), ((), ())), preferred_...  11.2 us
    dot_general x1, matrix products, body(): jnp.dot(lax.dynamic_index_in_dim(grad_cols, source, 0, keepdims=False), o...  9.23 us
    pallas_call x1, Pallas kernels, body(): pl.pallas_call(functools.partial(finish_kernel, heads, head_size), grid=(...  7.6 us
  transfers between devices with their start and end apart: 6, of which 3 were waited for; matrix products, arithmetic and copies ran while one was open for 21% of the time, Pallas kernels for 10%

profile of v1, /device:TPU:0, one launch (start us, length us, event | category | flops | bytes accessed | tf_op | source)
XLA Modules:
  0.0 289.3 jit_solution(9109502404342040896)
XLA Ops:
  7.2 0.7 all-gather.4.cloned.1.call-update
  7.9 101.6 %all-gather.4.cloned.1.call-done = bf16[1280,2560]{1,0:T(8,128)(2,1)} async-done(((bf16[80,2560]{1,0:T(8,128)(2,1)}), bf16[1280,2560]{1,0:T(8,128)(2,1)}) %all-gather.4.cloned.1.call-update) | async-done | bytes 6553616 | tf_op jit(solution)/shard_map/all_gather | solution.py:123
  109.6 3.0 %copy.71 = bf16[1,512,2560]{1,2,0:T(8,128)(2,1)S(1)} copy(bf16[1,512,2560]{2,1,0:T(8,128)(2,1)} %param.13) | data formatting | bytes 5242880 | tf_op args[0]
  112.6 1.7 copy.72
  114.4 1.2 reduce_window_sum.22
  117.1 2.3 copy.75
  119.4 0.8 copy.85
  121.9 19.9 %all-reduce = f32[320]{0:T(512)S(1)} all-reduce(f32[320]{0:T(512)S(1)} %dynamic-update-slice), channel_id=2, replica_groups=mesh['seq'=8,'lane'=2,'pair'=2] {'seq'}, use_global_device_ids=true, to_apply=%add | all-reduce | flops 320 | bytes 2560
  142.5 0.7 broadcast_in_dim.72
  143.3 0.7 broadcast_in_dim.76
  144.0 0.7 broadcast_in_dim.80
  144.7 2.3 copy.78
  147.5 2.3 copy.82
  149.8 2.2 copy.79
  152.1 2.3 copy.76
  157.5 0.9 convert_reduce_fusion
  158.4 7.0 %fusion.8 = f32[512,2560]{1,0:T(8,128)S(1)} fusion(bf16[1280,2560]{1,0:T(8,128)(2,1)} %all-gather.4.cloned.1.call-done, bf16[2,512,1280]{1,2,0:T(8,128)(2,1)} %bitcast.81, s32[]{:T(128)S(6)} %select_n.35), kind=kOutput, calls=%fused_computation.17 | convolution fusion | flops 3355443200 | bytes 13107204 | tf_op jit(solution)/shard_map/dot_general | solution.py:130
  165.5 9.2 %fusion.5.g_ref = bf16[512,2560]{1,0:T(8,128)(2,1)S(1)} fusion(f32[512,2560]{1,0:T(8,128)S(1)} %fusion.8, bf16[1280,2560]{1,0:T(8,128)(2,1)} %collective-permute-done, bf16[1,512,2560]{2,1,0:T(8,128)(2,1)S(1)} %copy-done.24, bf16[2,512,1280]{1,2,0:T(8,128)(2,1)S(1)} %bitcast.82, s32[]{:T(128)S(6)} %select_n.37), kind=kOutput, calls=%fused_computation.9 | convolution fusion | flops 3365928960 | bytes 18350084 | tf_op jit(solution)/shard_map/dot_general | solution.py:140
  174.7 6.9 %shard_map.141 = bf16[128,2560]{1,0:T(8,128)(2,1)} custom-call(bf16[512,2560]{1,0:T(8,128)(2,1)S(1)} %fusion.5.g_ref, f32[10,512,4]{2,1,0:T(8,128)S(1)} %bitcast.69, bf16[128,512]{1,0:T(8,128)(2,1)S(1)} %bitcast.75), custom_call_target="tpu_custom_call" | custom-call | flops 335544320 | bytes 2621440 | tf_op jit(solution)/shard_map/pallas_call | solution.py:198
  181.7 3.7 %all-to-all-start = ((bf16[8,16,2560]{2,1,0:T(8,128)(2,1)}), bf16[8,16,2560]{2,1,0:T(8,128)(2,1)S(1)}, u32[]{:S(2)}, u32[]{:S(2)}) async-start(bf16[8,16,2560]{2,1,0:T(8,128)(2,1)} %bitcast.23), calls=%async_computation | async-start | bytes 1310720 | tf_op jit(solution)/shard_map/all_to_all | solution.py:231
  185.4 1.2 fusion.35
  186.7 4.1 %multiply_bitcast_fusion = (f32[10,512,4]{2,1,0:T(8,128)S(1)}, f32[10,512,4]{2,1,0:T(8,128)S(1)}) fusion(f32[10,4,512]{1,2,0:T(8,128)} %copy.79, f32[10,4,512]{1,2,0:T(8,128)} %copy.82, f32[10,4,512]{1,2,0:T(8,128)} %copy.78), kind=kLoop, calls=%fused_computation.14 | loop fusion | flops 40960 | bytes 409600 | tf_op jit(solution)/shard_map/transpose | solution.py:92
  190.8 0.8 copy-done.9
  191.6 0.8 copy-done.10
  192.4 3.6 %pad_maximum_fusion.col_ref = f32[10,512,16]{2,1,0:T(8,128)} fusion(f32[10,512,4]{2,1,0:T(8,128)S(1)} %bitcast.77, f32[10,512,4]{2,1,0:T(8,128)S(1)} %get-tuple-element.10, f32[10,512,4]{2,1,0:T(8,128)S(1)} %bitcast.80, f32[10,512,4]{2,1,0:T(8,128)S(1)} %bitcast.79), kind=kLoop, calls=%fused_computation.13 | loop fusion | flops 245760 | bytes 655360 | tf_op jit(solution)/shard_map/concatenate | solution.py:163
  196.0 0.9 convolution_select_fusion.gram_ref
  196.9 20.1 %all-to-all-done = bf16[8,16,2560]{2,1,0:T(8,128)(2,1)S(1)} async-done(((bf16[8,16,2560]{2,1,0:T(8,128)(2,1)}), bf16[8,16,2560]{2,1,0:T(8,128)(2,1)S(1)}, u32[]{:S(2)}, u32[]{:S(2)}) %all-to-all-start) | async-done | bytes 655392 | tf_op jit(solution)/shard_map/all_to_all | solution.py:231
  217.1 1.5 fusion.15
  218.5 0.7 convert_dynamic-update-slice_fusion.4
  219.2 0.6 convert_dynamic-update-slice_fusion.3
  219.8 0.6 convert_dynamic-update-slice_fusion.2
  221.1 0.7 convert_dynamic-update-slice_fusion
  221.8 0.6 fusion.14
  222.4 0.6 broadcast_dynamic-update-slice_fusion
  223.1 3.5 %all-to-all-start.1 = ((bf16[8,16,2560]{2,1,0:T(8,128)(2,1)}), bf16[8,16,2560]{2,1,0:T(8,128)(2,1)S(1)}, u32[]{:S(2)}, u32[]{:S(2)}) async-start(bf16[8,16,2560]{2,1,0:T(8,128)(2,1)} %broadcast_dynamic-update-slice_fusion), calls=%async_computation.1 | async-start | bytes 1310720 | tf_op jit(solution)/shard_map/all_to_all | solution.py:240
  226.6 1.7 copy-done.1
  228.4 1.7 copy-done.2
  230.1 0.9 copy-done.6
  231.0 0.9 copy-done.7
  232.0 14.5 %shard_map.140.loc_ref = f32[512,2560]{1,0:T(8,128)} custom-call(bf16[512,2560]{1,0:T(8,128)(2,1)S(1)} %copy-done.1, f32[10,512,16]{2,1,0:T(8,128)S(1)} %copy-done.2, f32[10,4,512]{2,1,0:T(4,128)S(1)} %reshape_reshape.2.row_ref, f32[4,128,128]{2,1,0:T(8,128)S(1)} %copy-done.7, bf16[512,128]{1,0:T(8,128)(2,1)S(1)} %bitcast.73, bf16[128,512]{1,0:T(8,128)(2,1)S(1)} %bitcast.76, ...), custom_call_target="tpu_custom_call" | custom-call | flops 13421772800 | bytes 7864320 | tf_op jit(solution)/shard_map/pallas_call | solution.py:209
  246.4 7.6 %shard_map.142 = bf16[512,2560]{1,0:T(8,128)(2,1)S(1)} custom-call(f32[512,2560]{1,0:T(8,128)} %shard_map.140.loc_ref, f32[10,512,4]{2,1,0:T(8,128)S(1)} %get-tuple-element.9.col_ref, bf16[512,128]{1,0:T(8,128)(2,1)S(1)} %bitcast.74, bf16[128,2560]{1,0:T(8,128)(2,1)S(1)} %bitcast.70), custom_call_target="tpu_custom_call" | custom-call | flops 335544320 | bytes 7864320 | tf_op jit(solution)/shard_map/pallas_call | solution.py:244
  254.0 1.5 copy-done.3
  255.6 11.2 %fusion.4 = bf16[512,2560]{1,0:T(8,128)(2,1)S(1)} fusion(bf16[512,2560]{1,0:T(8,128)(2,1)} %copy-done.3, bf16[2560,2560]{1,0:T(8,128)(2,1)} %all-gather.6.cloned.1.call-done, bf16[1,512,2560]{2,1,0:T(8,128)(2,1)} %param.13), kind=kOutput, calls=%fused_computation.8 | convolution fusion | flops 6714818560 | bytes 20971520 | tf_op jit(solution)/shard_map/dot_general | solution.py:255
  266.8 0.7 gather_fusion
  267.7 0.7 reshape.378
  268.4 5.9 %all-to-all-start.2 = ((bf16[8,2,2560]{2,1,0:T(2,128)(2,1)}), bf16[8,2,2560]{2,1,0:T(2,128)(2,1)S(1)}, u32[]{:S(2)}, u32[]{:S(2)}) async-start(bf16[8,2,2560]{2,1,0:T(2,128)(2,1)} %reshape.378), calls=%async_computation.2 | async-start | bytes 163840 | tf_op jit(solution)/shard_map/all_to_all | solution.py:282
  274.6 6.7 %all-to-all-done.2 = bf16[8,2,2560]{2,1,0:T(2,128)(2,1)S(1)} async-done(((bf16[8,2,2560]{2,1,0:T(2,128)(2,1)}), bf16[8,2,2560]{2,1,0:T(2,128)(2,1)S(1)}, u32[]{:S(2)}, u32[]{:S(2)}) %all-to-all-start.2) | async-done | bytes 81952 | tf_op jit(solution)/shard_map/all_to_all | solution.py:282
  281.4 1.0 fusion.6
  (115 shorter events, 8.6 us)
Async XLA Ops:
  7.2 102.3 %all-gather.4.cloned.1.call-start = ((), (), s32[]{:S(2)}) async-start(), calls=%async_computation.3 | async-start | bytes 6963200 | tf_op jit(solution)/shard_map/all_gather | solution.py:123
  7.9 247.7 %all-gather.6.cloned.1.call-start = ((), (), s32[]{:S(2)}) async-start(), calls=%async_computation.4 | async-start | bytes 13516800 | tf_op jit(solution)/shard_map/all_gather | solution.py:125
  109.5 55.9 %collective-permute-start = (bf16[1280,2560]{1,0:T(8,128)(2,1)}, bf16[1280,2560]{1,0:T(8,128)(2,1)}, u32[]{:S(2)}, u32[]{:S(2)}) collective-permute-start(bf16[1280,2560]{1,0:T(8,128)(2,1)} %all-gather.4.cloned.1.call-done), channel_id=1, source_target_pairs={{1,0},{0,1},{3,2},{2,3},{5,4},{4,5},{7,6},{6,7},{9,8},{8,9},{11,10... | collective-permute-start | bytes 19660808 | tf_op jit(solution)/shard_map/ppermute | solution.py:136
  112.6 1.7 copy-start.15
  117.1 3.1 %copy-start.12 = (bf16[1,512,128]{2,1,0:T(8,128)(2,1)S(1)}, bf16[1,512,128]{2,1,0:T(8,128)(2,1)}, u32[]{:S(2)}) copy-start(bf16[1,512,128]{2,1,0:T(8,128)(2,1)} %param.18) | copy-start | bytes 393220
  117.1 3.2 %copy-start.29 = (u32[32]{0:T(128)S(1)}, u32[32]{0:T(128)}, u32[]{:S(2)}) copy-start(u32[32]{0:T(128)} %constant.77) | copy-start | bytes 388
  120.3 54.4 %copy-start.5 = (bf16[1,512,128]{1,2,0:T(8,128)(2,1)}, bf16[1,512,128]{1,2,0:T(8,128)(2,1)S(1)}, u32[]{:S(2)}) copy-start(bf16[1,512,128]{1,2,0:T(8,128)(2,1)S(1)} %copy.80) | copy-start | bytes 393220
  144.7 5.1 %copy-start.16 = (f32[1,40,512]{2,1,0:T(8,128)S(1)}, f32[1,40,512]{2,1,0:T(8,128)}, u32[]{:S(2)}) copy-start(f32[1,40,512]{2,1,0:T(8,128)} %param.20) | copy-start | bytes 245764
  149.8 4.6 %copy-start.23 = (f32[40]{0:T(128)S(1)}, f32[40]{0:T(128)}, u32[]{:S(2)}) copy-start(f32[40]{0:T(128)} %param.21) | copy-start | bytes 484
  149.8 4.7 %copy-start.17 = (s32[1,8,16]{2,1,0:T(8,128)S(1)}, s32[1,8,16]{2,1,0:T(8,128)}, u32[]{:S(2)}) copy-start(s32[1,8,16]{2,1,0:T(8,128)} %param.24) | copy-start | bytes 1540
  149.8 5.3 %copy-start.25 = (s32[1,8]{1,0:T(1,128)S(1)}, s32[1,8]{1,0:T(1,128)}, u32[]{:S(2)}) copy-start(s32[1,8]{1,0:T(1,128)} %param.23) | copy-start | bytes 100
  149.8 7.1 %copy-start.26 = (s32[1,1,16]{2,1,0:T(1,128)S(1)}, s32[1,1,16]{2,1,0:T(1,128)}, u32[]{:S(2)}) copy-start(s32[1,1,16]{2,1,0:T(1,128)} %param.22) | copy-start | bytes 196
  158.4 7.0 %copy-start.11 = (bf16[2,512,16,80]{1,3,2,0:T(8,128)(2,1)S(1)}, bf16[2,512,16,80]{1,3,2,0:T(8,128)(2,1)}, u32[]{:S(2)}) copy-start(bf16[2,512,16,80]{1,3,2,0:T(8,128)(2,1)} %copy.72) | copy-start | bytes 7864324
  158.4 7.1 %copy-start.24 = (bf16[1,512,2560]{2,1,0:T(8,128)(2,1)S(1)}, bf16[1,512,2560]{2,1,0:T(8,128)(2,1)}, u32[]{:S(2)}) copy-start(bf16[1,512,2560]{2,1,0:T(8,128)(2,1)} %param.16) | copy-start | bytes 7864324
  174.7 7.0 %copy-start = (bf16[512,2560]{1,0:T(8,128)(2,1)}, bf16[512,2560]{1,0:T(8,128)(2,1)S(1)}, u32[]{:S(2)}) copy-start(bf16[512,2560]{1,0:T(8,128)(2,1)S(1)} %fusion.5.g_ref) | copy-start | bytes 7864324
  181.7 35.2 %all-to-all-start = ((bf16[8,16,2560]{2,1,0:T(8,128)(2,1)}), bf16[8,16,2560]{2,1,0:T(8,128)(2,1)S(1)}, u32[]{:S(2)}, u32[]{:S(2)}) async-start(bf16[8,16,2560]{2,1,0:T(8,128)(2,1)} %bitcast.23), calls=%async_computation | async-start | bytes 1310720 | tf_op jit(solution)/shard_map/all_to_all | solution.py:231
  186.7 4.1 %copy-start.8 = (f32[10,4,512]{1,2,0:T(8,128)S(1)}, f32[10,4,512]{1,2,0:T(8,128)}, u32[]{:S(2)}) copy-start(f32[10,4,512]{1,2,0:T(8,128)} %copy.79) | copy-start | bytes 245764
  186.7 4.9 %copy-start.9 = (f32[10,4,512]{1,2,0:T(8,128)S(1)}, f32[10,4,512]{1,2,0:T(8,128)}, u32[]{:S(2)}) copy-start(f32[10,4,512]{1,2,0:T(8,128)} %copy.75) | copy-start | bytes 245764
  186.7 5.7 %copy-start.10 = (f32[10,4,512]{1,2,0:T(8,128)S(1)}, f32[10,4,512]{1,2,0:T(8,128)}, u32[]{:S(2)}) copy-start(f32[10,4,512]{1,2,0:T(8,128)} %copy.76) | copy-start | bytes 245764
  192.4 3.6 %copy-start.4 = (bf16[1,512,128]{2,1,0:T(8,128)(2,1)S(1)}, bf16[1,512,128]{2,1,0:T(8,128)(2,1)}, u32[]{:S(2)}) copy-start(bf16[1,512,128]{2,1,0:T(8,128)(2,1)} %param.17) | copy-start | bytes 393220
  192.4 3.6 %copy-start.13 = (bf16[1,512,128]{2,1,0:T(8,128)(2,1)S(1)}, bf16[1,512,128]{2,1,0:T(8,128)(2,1)}, u32[]{:S(2)}) copy-start(bf16[1,512,128]{2,1,0:T(8,128)(2,1)} %param.18) | copy-start | bytes 393220
  223.1 23.3 %all-to-all-start.1 = ((bf16[8,16,2560]{2,1,0:T(8,128)(2,1)}), bf16[8,16,2560]{2,1,0:T(8,128)(2,1)S(1)}, u32[]{:S(2)}, u32[]{:S(2)}) async-start(bf16[8,16,2560]{2,1,0:T(8,128)(2,1)} %broadcast_dynamic-update-slice_fusion), calls=%async_computation.1 | async-start | bytes 1310720 | tf_op jit(solution)/shard_map/all_to_all | solution.py:240
  226.6 1.7 copy-start.1
  228.4 1.7 copy-start.2
  230.1 0.9 copy-start.6
  231.0 0.9 copy-start.7
  254.0 1.5 copy-start.3
  255.5 12.0 %copy-start.20 = (s32[16]{0:T(128)S(1)}, s32[16]{0:T(128)}, u32[]{:S(2)}) copy-start(s32[16]{0:T(128)} %fusion.35) | copy-start | bytes 196
  255.5 12.0 %copy-start.21 = (pred[16]{0:T(512)(128)(4,1)S(1)}, pred[16]{0:T(512)(128)(4,1)}, u32[]{:S(2)}) copy-start(pred[16]{0:T(512)(128)(4,1)} %dynamic-slice_bitcast_fusion) | copy-start | bytes 52
  255.5 18.8 %copy-start.18 = (s32[8,16]{1,0:T(8,128)S(1)}, s32[8,16]{1,0:T(8,128)}, u32[]{:S(2)}) copy-start(s32[8,16]{1,0:T(8,128)} %convert_reduce_fusion) | copy-start | bytes 1540
  255.5 18.8 %copy-start.22 = (s32[8]{0:T(128)S(1)}, s32[8]{0:T(128)}, u32[]{:S(2)}) copy-start(s32[8]{0:T(128)} %iota_multiply_fusion) | copy-start | bytes 100
  255.5 19.0 %copy-start.19 = (s32[1,8,16]{2,1,0:T(8,128)S(1)}, s32[1,8,16]{2,1,0:T(8,128)}, u32[]{:S(2)}) copy-start(s32[1,8,16]{2,1,0:T(8,128)} %param.25) | copy-start | bytes 1540
  255.5 19.1 %copy-start.27 = (pred[128]{0:T(512)(128)(4,1)S(1)}, pred[128]{0:T(512)(128)(4,1)}, u32[]{:S(2)}) copy-start(pred[128]{0:T(512)(128)(4,1)} %eq.77) | copy-start | bytes 388
  255.5 19.1 %copy-start.28 = (pred[128]{0:T(512)(128)(4,1)S(1)}, pred[128]{0:T(512)(128)(4,1)}, u32[]{:S(2)}) copy-start(pred[128]{0:T(512)(128)(4,1)} %lt.82) | copy-start | bytes 388
  266.8 15.7 %copy-start.14 = (bf16[512,2560]{1,0:T(8,128)(2,1)}, bf16[512,2560]{1,0:T(8,128)(2,1)S(1)}, u32[]{:S(2)}) copy-start(bf16[512,2560]{1,0:T(8,128)(2,1)S(1)} %fusion.4) | copy-start | bytes 7864324
  268.4 12.9 %all-to-all-start.2 = ((bf16[8,2,2560]{2,1,0:T(2,128)(2,1)}), bf16[8,2,2560]{2,1,0:T(2,128)(2,1)S(1)}, u32[]{:S(2)}, u32[]{:S(2)}) async-start(bf16[8,2,2560]{2,1,0:T(2,128)(2,1)} %reshape.378), calls=%async_computation.2 | async-start | bytes 163840 | tf_op jit(solution)/shard_map/all_to_all | solution.py:282
Sparse Core Ops, SparseCore 0:
  10.9 98.5 all-gather.3
  112.3 108.3 all-gather.5

commit v2 on v1

--- a/solution.py
+++ b/solution.py
@@ -109,8 +109,6 @@
 ):
     seq_count = lax.axis_size("seq")
     seq_index = lax.axis_index("seq")
-    lane_count = lax.axis_size("lane")
-    pair_count = lax.axis_size("pair")
     grad_rows = grad_top[0]
     tok_rows, model_width = grad_rows.shape
     head_count = log_decay.shape[1]
@@ -118,31 +116,6 @@
     head_size = inner_width // head_count
     state_width = write_vec.shape[2]
     slot_count = visual_owner.shape[2]
-    weight_rows = out_weight.shape[0]
-
-    held = lax.all_gather(out_weight, ("seq", "lane"), axis=0, tiled=True)
-    in_part, held = lax.optimization_barrier((in_weight, held))
-    in_full = lax.all_gather(in_part, ("seq", "lane", "pair"), axis=0, tiled=True)
-    pair_index = lax.axis_index("pair")
-    grad_cols = grad_rows.reshape(
-        tok_rows, seq_count * lane_count, pair_count, weight_rows
-    ).transpose(2, 0, 1, 3).reshape(pair_count, tok_rows, -1)
-    out_value = jnp.dot(
-        lax.dynamic_index_in_dim(grad_cols, pair_index, 0, keepdims=False),
-        held,
-        preferred_element_type=jnp.float32,
-    )
-    for shift in range(1, pair_count):
-        other = lax.ppermute(
-            held, "pair", [((i + shift) % pair_count, i) for i in range(pair_count)]
-        )
-        source = (pair_index + shift) % pair_count
-        out_value += jnp.dot(
-            lax.dynamic_index_in_dim(grad_cols, source, 0, keepdims=False),
-            other,
-            preferred_element_type=jnp.float32,
-        )
-    gated = (out_value * jax.nn.silu(gate_branch[0].astype(jnp.float32))).astype(jnp.bfloat16)
 
     length = min(BLOCK, tok_rows)
     blocks = tok_rows // length
@@ -183,6 +156,28 @@
     )
     place = jnp.arange(length)
     gram = jnp.where(place[None, None, :] >= place[None, :, None], gram, 0.0)
+
+    skip_decays = jnp.repeat(jnp.exp(lax.all_gather(device_decay, "seq")), head_size, axis=1)
+
+    out_full = lax.all_gather(out_weight, ("seq", "lane", "pair"), axis=0, tiled=True)
+    in_part, out_full, lead_cols, local_cols, last_cols, cum_rows, gram, read_t, decays = (
+        lax.optimization_barrier(
+            (
+                in_weight,
+                out_full,
+                lead_cols,
+                local_cols,
+                last_cols,
+                cum_rows,
+                gram,
+                read_t,
+                skip_decays,
+            )
+        )
+    )
+    in_full = lax.all_gather(in_part, ("seq", "lane", "pair"), axis=0, tiled=True)
+    out_value = jnp.dot(grad_rows, out_full, preferred_element_type=jnp.float32)
+    gated = (out_value * jax.nn.silu(gate_branch[0].astype(jnp.float32))).astype(jnp.bfloat16)
 
     wide = pl.BlockSpec((tok_rows, width), lambda i: (0, i))
     state_spec = pl.BlockSpec((state_width, width), lambda i: (0, i))
@@ -226,8 +221,6 @@
         ),
     )(gated, local_cols, cum_rows, gram, write_rows, read_t, skip_row)
 
-    decays = jnp.exp(lax.all_gather(device_decay, "seq"))
-    decays = jnp.repeat(decays, head_size, axis=1)
     shares = lax.all_to_all(
         contrib.reshape(seq_count, -1, inner_width), "seq", split_axis=0, concat_axis=0, tiled=True
     ).astype(jnp.float32)
@@ -252,11 +245,8 @@
             flops=state_flops, bytes_accessed=gated.size * 6, transcendentals=0
         ),
     )(local, last_cols, write_rows, inflow)
-    back = lax.dot_general(
-        inner_grad, in_full, (((1,), (1,)), ((), ())), preferred_element_type=jnp.float32
-    )
-    result = (grad_rows.astype(jnp.float32) + back).astype(jnp.bfloat16)
-    own_rows = result[visual_pos[0, 0]]
+    place = visual_pos[0, 0]
+    own_rows = jnp.concatenate([inner_grad[place], grad_rows[place]], axis=1)
     owner_row = visual_owner[0]
     patch_row = visual_patch[0]
     count_row = visual_count[0]
@@ -278,7 +268,7 @@
         jnp.bfloat16
     )
     send_rows = jnp.dot(send_map, own_rows, preferred_element_type=jnp.float32).astype(jnp.bfloat16)
-    send_rows = send_rows.reshape(seq_count, CAP, model_width)
+    send_rows = send_rows.reshape(seq_count, CAP, inner_width + model_width)
     landed = lax.all_to_all(send_rows, "seq", split_axis=0, concat_axis=0, tiled=True)
     mine_mask = live_slot & (owner_row == seq_index)
     column = jnp.arange(seq_count)[:, None] * CAP + rank_row
@@ -291,9 +281,19 @@
     select = lax.dot_general(
         patch_hit, column_hit, (((0,), (0,)), ((), ())), preferred_element_type=jnp.float32
     ).astype(jnp.bfloat16)
-    patches = jnp.dot(
-        select, landed.reshape(seq_count * CAP, model_width), preferred_element_type=jnp.float32
+    patch_rows = jnp.dot(
+        select, landed.reshape(seq_count * CAP, -1), preferred_element_type=jnp.float32
     ).astype(jnp.bfloat16)
+    inner_grad, patch_rows, in_full = lax.optimization_barrier((inner_grad, patch_rows, in_full))
+
+    def project(inner_rows, top_rows):
+        back = lax.dot_general(
+            inner_rows, in_full, (((1,), (1,)), ((), ())), preferred_element_type=jnp.float32
+        )
+        return (top_rows.astype(jnp.float32) + back).astype(jnp.bfloat16)
+
+    result = project(inner_grad, grad_rows)
+    patches = project(patch_rows[:, :inner_width], patch_rows[:, inner_width:])
     return (result[None], patches[None])
 
 

time: 290 us -> 260 us (0.90)
  waiting for transfers between devices: 129 us -> 98.6 us
  matrix products: 29.6 us -> 33.9 us
  blocking collectives: 19.9 us -> 23.7 us
  other arithmetic: 18.2 us -> 14.4 us
  local copies, waits for them, and re-layouts: 35 us -> 31.7 us
    all_gather x1, waiting for transfers between devices: 102 us -> 55.5 us  [body(): lax.all_gather(out_weight, ('seq', 'lane', 'pair'), axis=0, tiled=True)]
    all_to_all x1, waiting for transfers between devices: 0.01 us -> 13.7 us  [body(): lax.all_to_all(arriving, 'seq', split_axis=0, concat_axis=0, tiled=True)]
    gather x1 -> x2, local copies, waits for them, and re-layouts: 0.72 us -> 6.15 us  [body(): own_rows = jnp.concatenate([inner_grad[place], grad_rows[place]], axis=1)]
    unnamed x65 -> x44, local copies, waits for them, and re-layouts: 12.5 us -> 8.62 us
    unnamed x1, blocking collectives: 19.9 us -> 23.7 us
    dot_general x4, matrix products: 28.5 us -> 31.9 us  [the longest x2 20.1 us: project(): lax.dot_general(inner_rows, in_full, (((1,), (1,)), ((), ())), preferred_...]
    transpose x1 -> x2, other arithmetic: 4.07 us -> 6.29 us  [by_step(): return x.reshape(-1, per, x.shape[1]).transpose(0, 2, 1)]
  transfers between devices with their start and end apart: 6 -> 5, of which waited for: 3 -> 4; matrix products, arithmetic and copies ran while one was open for 21% -> 20% of each run, Pallas kernels for 10% -> 11%
where the time goes in v2:
time: 260 us; the launch traced here: 259 us
  waiting for transfers between devices  98.6 us (38%)
  matrix products  33.9 us (13%)
  local copies, waits for them, and re-layouts  31.7 us (12%)
  Pallas kernels  29 us (11%)
  blocking collectives  23.7 us (9%)
  between operations  15.1 us (6%)
  other arithmetic  14.4 us (6%)
  starting transfers between devices  12.8 us (5%)
    all_gather x1, waiting for transfers between devices, body(): lax.all_gather(out_weight, ('seq', 'lane', 'pair'), axis=0, tiled=True)  55.5 us
    unnamed x1, blocking collectives  23.7 us
    all_to_all x1, waiting for transfers between devices, body(): lax.all_to_all(contrib.reshape(seq_count, -1, inner_width), 'seq', split_...  21.4 us
    dot_general x2, matrix products, project(): lax.dot_general(inner_rows, in_full, (((1,), (1,)), ((), ())), preferred_...  20.1 us
    pallas_call x1, Pallas kernels, body(): pl.pallas_call(functools.partial(local_kernel, heads, head_size), grid=(s...  14.5 us
    all_to_all x1, waiting for transfers between devices, body(): lax.all_to_all(arriving, 'seq', split_axis=0, concat_axis=0, tiled=True)  13.7 us
    dot_general x1, matrix products, body(): out_value = jnp.dot(grad_rows, out_full, preferred_element_type=jnp.float32)  11.4 us
    unnamed x44, local copies, waits for them, and re-layouts  8.62 us
  transfers between devices with their start and end apart: 5, of which 4 were waited for; matrix products, arithmetic and copies ran while one was open for 20% of the time, Pallas kernels for 11%

profile of v2, /device:TPU:0, one launch (start us, length us, event | category | flops | bytes accessed | tf_op | source)
XLA Modules:
  0.0 259.1 jit_solution(2013358203591069302)
XLA Ops:
  7.2 0.7 all-gather.4.cloned.1.call-update
  8.0 0.9 reshape_squeeze.12
  8.9 1.2 reduce_window_sum.24
  10.2 0.3 copy.82
  11.6 0.7 exponential_bitcast_fusion.1
  12.3 0.8 copy.73
  13.6 2.3 copy.76
  15.9 2.3 copy.77
  18.2 5.6 %multiply_bitcast_fusion = (f32[10,512,4]{2,1,0:T(8,128)}, f32[10,512,4]{2,1,0:T(8,128)}) fusion(f32[10,4,512]{1,2,0:T(8,128)} %copy.77, f32[10,4,512]{1,2,0:T(8,128)} %copy.76, f32[10,4,512]{1,2,0:T(8,128)S(1)} %copy.73), kind=kLoop, calls=%fused_computation.16 | loop fusion | flops 40960 | bytes 409600 | tf_op jit(solution)/shard_map/transpose | solution.py:92
  23.8 3.2 %copy.74 = f32[10,512,4]{1,2,0:T(4,128)} copy(f32[10,512,4]{2,1,0:T(8,128)} %get-tuple-element.37) | data formatting | bytes 163840 | tf_op jit(solution)/shard_map/transpose | solution.py:92
  27.0 0.8 copy.71
  27.8 0.6 dynamic-slice.1
  29.2 23.7 %all-reduce = f32[320]{0:T(512)S(1)} all-reduce(f32[320]{0:T(512)S(1)} %dynamic-update-slice), channel_id=2, replica_groups=mesh['seq'=8,'lane'=2,'pair'=2] {'seq'}, use_global_device_ids=true, to_apply=%add | all-reduce | flops 320 | bytes 2560
  53.2 0.8 reshape.342
  54.1 1.0 pad_maximum_fusion
  55.2 0.9 convolution_select_fusion.gram_ref
  56.1 55.5 %all-gather.4.cloned.1.call-done = bf16[2560,2560]{1,0:T(8,128)(2,1)} async-done(((bf16[80,2560]{1,0:T(8,128)(2,1)}), bf16[2560,2560]{1,0:T(8,128)(2,1)}) %all-gather.4.cloned.1.call-update) | async-done | bytes 13107216 | tf_op jit(solution)/shard_map/all_gather | solution.py:162
  111.6 11.4 %fusion.4.g_ref = bf16[512,2560]{1,0:T(8,128)(2,1)S(1)} fusion(bf16[2560,2560]{1,0:T(8,128)(2,1)} %all-gather.4.cloned.1.call-done, bf16[1,512,2560]{2,1,0:T(8,128)(2,1)} %param.16, bf16[1,512,2560]{2,1,0:T(8,128)(2,1)} %param.13), kind=kOutput, calls=%fused_computation.11 | convolution fusion | flops 6720061440 | bytes 20971520 | tf_op jit(solution)/shard_map/dot_general | solution.py:179
  123.1 6.9 %shard_map.141 = bf16[128,2560]{1,0:T(8,128)(2,1)} custom-call(bf16[512,2560]{1,0:T(8,128)(2,1)S(1)} %fusion.4.g_ref, f32[10,512,4]{2,1,0:T(8,128)S(1)} %bitcast.59, bf16[128,512]{1,0:T(8,128)(2,1)S(1)} %bitcast.65), custom_call_target="tpu_custom_call" | custom-call | flops 335544320 | bytes 2621440 | tf_op jit(solution)/shard_map/pallas_call | solution.py:193
  130.0 4.1 %all-to-all-start = ((bf16[8,16,2560]{2,1,0:T(8,128)(2,1)}), bf16[8,16,2560]{2,1,0:T(8,128)(2,1)S(1)}, u32[]{:S(2)}, u32[]{:S(2)}) async-start(bf16[8,16,2560]{2,1,0:T(8,128)(2,1)} %bitcast.19), calls=%async_computation | async-start | bytes 1310720 | tf_op jit(solution)/shard_map/all_to_all | solution.py:224
  134.5 3.4 %gather_fusion.1 = bf16[16,2560]{1,0:T(8,128)(2,1)} fusion(bf16[512,2560]{1,0:T(8,128)(2,1)} %bitcast.69, s32[1024]{0:T(1024)S(1)} %pad_clamp_fusion), kind=kCustom, calls=%fused_computation.1 | custom fusion | bytes 163904 | tf_op jit(solution)/shard_map/gather | solution.py:249
  138.2 2.2 copy.80.col_ref
  140.7 21.4 %all-to-all-done = bf16[8,16,2560]{2,1,0:T(8,128)(2,1)S(1)} async-done(((bf16[8,16,2560]{2,1,0:T(8,128)(2,1)}), bf16[8,16,2560]{2,1,0:T(8,128)(2,1)S(1)}, u32[]{:S(2)}, u32[]{:S(2)}) %all-to-all-start) | async-done | bytes 655392 | tf_op jit(solution)/shard_map/all_to_all | solution.py:224
  162.2 0.7 fusion.14
  162.9 0.7 convert_dynamic-update-slice_fusion.4
  163.6 0.6 convert_dynamic-update-slice_fusion.3
  164.2 0.6 convert_dynamic-update-slice_fusion.2
  164.9 0.6 convert_dynamic-update-slice_fusion.1
  165.5 0.7 convert_dynamic-update-slice_fusion
  166.2 0.6 fusion.13
  166.8 0.6 broadcast_dynamic-update-slice_fusion
  167.4 4.6 %all-to-all-start.1 = ((bf16[8,16,2560]{2,1,0:T(8,128)(2,1)}), bf16[8,16,2560]{2,1,0:T(8,128)(2,1)S(1)}, u32[]{:S(2)}, u32[]{:S(2)}) async-start(bf16[8,16,2560]{2,1,0:T(8,128)(2,1)} %broadcast_dynamic-update-slice_fusion), calls=%async_computation.1 | async-start | bytes 1310720 | tf_op jit(solution)/shard_map/all_to_all | solution.py:233
  172.0 1.7 copy-done.4
  173.8 2.5 copy-done.5
  176.3 0.9 copy-done.8
  177.2 0.9 copy-done.9
  178.2 14.5 %shard_map.140.loc_ref = f32[512,2560]{1,0:T(8,128)} custom-call(bf16[512,2560]{1,0:T(8,128)(2,1)S(1)} %copy-done.4, f32[10,512,16]{2,1,0:T(8,128)S(1)} %copy-done.5, f32[10,4,512]{2,1,0:T(4,128)S(1)} %reduce_window_sum.25.row_ref, f32[4,128,128]{2,1,0:T(8,128)S(1)} %copy-done.9, bf16[512,128]{1,0:T(8,128)(2,1)S(1)} %bitcast.63, ...), custom_call_target="tpu_custom_call" | custom-call | flops 13421772800 | bytes 7864320 | tf_op jit(solution)/shard_map/pallas_call | solution.py:204
  192.6 13.7 %all-to-all-done.1 = bf16[8,16,2560]{2,1,0:T(8,128)(2,1)S(1)} async-done(((bf16[8,16,2560]{2,1,0:T(8,128)(2,1)}), bf16[8,16,2560]{2,1,0:T(8,128)(2,1)S(1)}, u32[]{:S(2)}, u32[]{:S(2)}) %all-to-all-start.1) | async-done | bytes 655392 | tf_op jit(solution)/shard_map/all_to_all | solution.py:233
  206.3 7.6 %shard_map.142 = bf16[512,2560]{1,0:T(8,128)(2,1)S(1)} custom-call(f32[512,2560]{1,0:T(8,128)} %shard_map.140.loc_ref, f32[10,512,4]{2,1,0:T(8,128)S(1)} %copy-done, bf16[512,128]{1,0:T(8,128)(2,1)S(1)} %bitcast.64, bf16[128,2560]{1,0:T(8,128)(2,1)S(1)} %bitcast.60), custom_call_target="tpu_custom_call" | custom-call | flops 335544320 | bytes 7864320 | tf_op jit(solution)/shard_map/pallas_call | solution.py:237
  214.0 1.5 copy-done.1
  215.5 2.8 %gather_fusion = bf16[16,2560]{1,0:T(8,128)(2,1)S(1)} fusion(bf16[512,2560]{1,0:T(8,128)(2,1)} %copy-done.1, s32[1024]{0:T(1024)S(1)} %pad_clamp_fusion), kind=kCustom, calls=%fused_computation | custom fusion | bytes 163904 | tf_op jit(solution)/shard_map/gather | solution.py:249
  218.2 1.1 convolution_convert_fusion.1
  219.3 0.7 reshape.345
  220.0 4.0 %all-to-all-start.2 = ((bf16[8,2,5120]{2,1,0:T(2,128)(2,1)}), bf16[8,2,5120]{2,1,0:T(2,128)(2,1)S(1)}, u32[]{:S(2)}, u32[]{:S(2)}) async-start(bf16[8,2,5120]{2,1,0:T(2,128)(2,1)} %reshape.345), calls=%async_computation.2 | async-start | bytes 327680 | tf_op jit(solution)/shard_map/all_to_all | solution.py:272
  224.3 7.3 %all-to-all-done.2 = bf16[8,2,5120]{2,1,0:T(2,128)(2,1)S(1)} async-done(((bf16[8,2,5120]{2,1,0:T(2,128)(2,1)}), bf16[8,2,5120]{2,1,0:T(2,128)(2,1)S(1)}, u32[]{:S(2)}, u32[]{:S(2)}) %all-to-all-start.2) | async-done | bytes 163872 | tf_op jit(solution)/shard_map/all_to_all | solution.py:272
  231.7 0.4 convolution_convert_fusion
  232.2 9.0 %fusion.7 = bf16[1,16,2560]{2,1,0:T(8,128)(2,1)} fusion(bf16[2560,2560]{1,0:T(8,128)(2,1)} %all-gather.6.cloned.1.call-done, bf16[16,5120]{1,0:T(8,128)(2,1)S(1)} %convolution_convert_fusion), kind=kOutput, calls=%fused_computation.15 | convolution fusion | flops 209838080 | bytes 13352960 | tf_op jit(solution)/shard_map/dot_general | solution.py:290
  241.2 11.1 %fusion.5 = bf16[1,512,2560]{2,1,0:T(8,128)(2,1)} fusion(bf16[512,2560]{1,0:T(8,128)(2,1)S(1)} %copy-done.2, bf16[2560,2560]{1,0:T(8,128)(2,1)} %all-gather.6.cloned.1.call-done, bf16[1,512,2560]{2,1,0:T(8,128)(2,1)S(1)} %copy-done.12), kind=kOutput, calls=%fused_computation.12 | convolution fusion | flops 6714818560 | bytes 20971520 | tf_op jit(solution)/shard_map/dot_general | solution.py:290
  (81 shorter events, 3.8 us)
Async XLA Ops:
  7.2 104.4 %all-gather.4.cloned.1.call-start = ((), (), s32[]{:S(2)}) async-start(), calls=%async_computation.3 | async-start | bytes 13516800 | tf_op jit(solution)/shard_map/all_gather | solution.py:162
  7.9 224.3 %all-gather.6.cloned.1.call-start = ((), (), s32[]{:S(2)}) async-start(), calls=%async_computation.4 | async-start | bytes 13516800 | tf_op jit(solution)/shard_map/all_gather | solution.py:178
  12.3 3.6 %copy-start.13 = (f32[1,40,512]{2,1,0:T(8,128)S(1)}, f32[1,40,512]{2,1,0:T(8,128)}, u32[]{:S(2)}) copy-start(f32[1,40,512]{2,1,0:T(8,128)} %param.20) | copy-start | bytes 245764
  23.8 4.0 %copy-start.19 = (u32[32]{0:T(128)S(1)}, u32[32]{0:T(128)}, u32[]{:S(2)}) copy-start(u32[32]{0:T(128)} %constant.55) | copy-start | bytes 388
  23.8 30.2 %copy-start.10 = (bf16[1,512,128]{2,1,0:T(8,128)(2,1)S(1)}, bf16[1,512,128]{2,1,0:T(8,128)(2,1)}, u32[]{:S(2)}) copy-start(bf16[1,512,128]{2,1,0:T(8,128)(2,1)} %param.18) | copy-start | bytes 393220
  26.9 28.2 %copy-start.6 = (bf16[1,512,128]{2,1,0:T(8,128)(2,1)S(1)}, bf16[1,512,128]{2,1,0:T(8,128)(2,1)}, u32[]{:S(2)}) copy-start(bf16[1,512,128]{2,1,0:T(8,128)(2,1)} %param.17) | copy-start | bytes 393220
  27.0 84.6 %copy-start.14 = (s32[1,8,16]{2,1,0:T(8,128)S(1)}, s32[1,8,16]{2,1,0:T(8,128)}, u32[]{:S(2)}) copy-start(s32[1,8,16]{2,1,0:T(8,128)} %param.24) | copy-start | bytes 1540
  54.1 68.9 %copy-start.7 = (bf16[1,512,128]{1,2,0:T(8,128)(2,1)}, bf16[1,512,128]{1,2,0:T(8,128)(2,1)S(1)}, u32[]{:S(2)}) copy-start(bf16[1,512,128]{1,2,0:T(8,128)(2,1)S(1)} %copy.78) | copy-start | bytes 393220
  123.0 6.9 %copy-start.3 = (bf16[512,2560]{1,0:T(8,128)(2,1)}, bf16[512,2560]{1,0:T(8,128)(2,1)S(1)}, u32[]{:S(2)}) copy-start(bf16[512,2560]{1,0:T(8,128)(2,1)S(1)} %fusion.4.g_ref) | copy-start | bytes 7864324
  123.0 11.1 %copy-start.16 = (f32[40]{0:T(128)S(1)}, f32[40]{0:T(128)}, u32[]{:S(2)}) copy-start(f32[40]{0:T(128)} %param.21) | copy-start | bytes 484
  123.0 11.3 %copy-start.17 = (s32[1,8]{1,0:T(1,128)S(1)}, s32[1,8]{1,0:T(1,128)}, u32[]{:S(2)}) copy-start(s32[1,8]{1,0:T(1,128)} %param.23) | copy-start | bytes 100
  123.0 11.5 %copy-start.18 = (s32[1,1,16]{2,1,0:T(1,128)S(1)}, s32[1,1,16]{2,1,0:T(1,128)}, u32[]{:S(2)}) copy-start(s32[1,1,16]{2,1,0:T(1,128)} %param.22) | copy-start | bytes 196
  130.0 10.5 %copy-start.11 = (f32[8,2560]{1,0:T(8,128)S(1)}, f32[8,2560]{1,0:T(8,128)}, u32[]{:S(2)}) copy-start(f32[8,2560]{1,0:T(8,128)} %reshape.342) | copy-start | bytes 245764
  130.0 32.1 %all-to-all-start = ((bf16[8,16,2560]{2,1,0:T(8,128)(2,1)}), bf16[8,16,2560]{2,1,0:T(8,128)(2,1)S(1)}, u32[]{:S(2)}, u32[]{:S(2)}) async-start(bf16[8,16,2560]{2,1,0:T(8,128)(2,1)} %bitcast.19), calls=%async_computation | async-start | bytes 1310720 | tf_op jit(solution)/shard_map/all_to_all | solution.py:224
  167.4 38.9 %all-to-all-start.1 = ((bf16[8,16,2560]{2,1,0:T(8,128)(2,1)}), bf16[8,16,2560]{2,1,0:T(8,128)(2,1)S(1)}, u32[]{:S(2)}, u32[]{:S(2)}) async-start(bf16[8,16,2560]{2,1,0:T(8,128)(2,1)} %broadcast_dynamic-update-slice_fusion), calls=%async_computation.1 | async-start | bytes 1310720 | tf_op jit(solution)/shard_map/all_to_all | solution.py:233
  172.0 1.7 copy-start.4
  173.8 2.5 copy-start.5
  176.3 0.9 copy-start.8
  177.2 0.9 copy-start.9
  178.1 28.2 %copy-start = (f32[10,512,4]{2,1,0:T(8,128)S(1)}, f32[10,512,4]{2,1,0:T(8,128)}, u32[]{:S(2)}) copy-start(f32[10,512,4]{2,1,0:T(8,128)} %get-tuple-element.19.col_ref) | copy-start | bytes 245764
  206.3 17.9 %copy-start.15 = (s32[1,8,16]{2,1,0:T(8,128)S(1)}, s32[1,8,16]{2,1,0:T(8,128)}, u32[]{:S(2)}) copy-start(s32[1,8,16]{2,1,0:T(8,128)} %param.25) | copy-start | bytes 1540
  214.0 1.5 copy-start.1
  220.0 11.6 %all-to-all-start.2 = ((bf16[8,2,5120]{2,1,0:T(2,128)(2,1)}), bf16[8,2,5120]{2,1,0:T(2,128)(2,1)S(1)}, u32[]{:S(2)}, u32[]{:S(2)}) async-start(bf16[8,2,5120]{2,1,0:T(2,128)(2,1)} %reshape.345), calls=%async_computation.2 | async-start | bytes 327680 | tf_op jit(solution)/shard_map/all_to_all | solution.py:272
  232.1 9.1 %copy-start.2 = (bf16[512,2560]{1,0:T(8,128)(2,1)S(1)}, bf16[512,2560]{1,0:T(8,128)(2,1)}, u32[]{:S(2)}) copy-start(bf16[512,2560]{1,0:T(8,128)(2,1)} %copy-done.1) | copy-start | bytes 7864324
  232.2 9.0 %copy-start.12 = (bf16[1,512,2560]{2,1,0:T(8,128)(2,1)S(1)}, bf16[1,512,2560]{2,1,0:T(8,128)(2,1)}, u32[]{:S(2)}) copy-start(bf16[1,512,2560]{2,1,0:T(8,128)(2,1)} %param.13) | copy-start | bytes 7864324
Sparse Core Ops, SparseCore 0:
  10.8 100.6 all-gather.3
  114.4 112.7 all-gather.5
